TPU v7x, 32 devices: a whole 2x2x4 slice. The times are simulated.
32 devices in a mesh: rel: 4 (over x, core), dst: 4 (over z), mp: 2 (over y).
Axes of the slice: x: 2, y: 2, z: 4, core: 2. Of those that a mesh axis runs over, the one named last changes fastest.
Arguments:
- node_table: bfloat16 [16384, 512], P(('rel', 'dst')), may hold values from -6 to 6
- edge_weights: bfloat16 [4, 32, 128, 128], P('rel', 'dst'), may hold values from -0.5 to 0.5
- src_ids: int32 [4, 32, 128], P('rel', 'dst'), may hold values from 0 to 1023
- dst_ids: int32 [4, 32, 128], P('rel', 'dst'), may hold values from 0 to 511
- block_mask: int32 [4, 32], P('rel', 'dst'), may hold values 0 or 1
- basis_coef: float32 [4, 32], P('rel'), may hold values from -0.375 to 0.375
- basis_mats: bfloat16 [32, 512, 512], P(None, None, 'mp'), may hold values from -0.25 to 0.25
- type_bias: float32 [4, 512], P(None, 'mp'), may hold values from -3 to 3
- type_rows: int32 [4], replicated, may hold values from 1 to 256, 512 in all
- cotangent: bfloat16 [2048, 512], P(('rel', 'dst'), 'mp'), may hold values from -0.005859375 to 0.005859375
Outputs:
- layer_out: bfloat16 [2048, 512], P(('rel', 'dst'), 'mp')
- coef_grad: float32 [4, 32], P('rel')
Inputs may be any that keep to these rules, and one draw needn't show every extreme that they name: `type_rows`: the 4 counts sum to 512.
All inputs are finite; a program needn't handle non-finite values. No bound on the sum of `block_mask` on one device may be relied on, other than what follows from the above.
Results may differ from a plain program's by a relative error of at most 0.0062.
Values may be sent and summed in bfloat16 or wider, within the bound.
No kernel may reach another device: no remote copies, remote signals or barrier semaphores. Data moves between devices by JAX's collectives and lax.ppermute only.
A program may use at most 64 MiB of HBM per device.

v0:
```python
import functools
import jax
import jax.numpy as jnp
from jax import lax
from jax.experimental import pallas as pl
from jax.experimental.pallas import tpu as pltpu
from jax.sharding import PartitionSpec as P


f32, bf16, i32 = jnp.float32, jnp.bfloat16, jnp.int32
LIMIT = 40 * 1024 * 1024
FIRST_FLOPS = 20_000_000_000
MIX = 4
CONTRACT_ROWS = (((0,), (0,)), ((), ()))


def whole(space=pltpu.VMEM):
    return pl.BlockSpec(memory_space=space)


def spread_rows(row, rows):
    return jnp.broadcast_to(row, (rows, rows)).T


def one_hot(column, width):
    rows, lanes = column.shape
    lane = lax.broadcasted_iota(i32, (rows, lanes), 1)
    parts = [(column == lane + c).astype(bf16) for c in range(0, width, lanes)]
    return jnp.concatenate(parts, axis=1)


def mix(coef, basis, acc, begin, end):
    features = acc.shape[0]
    size, chunk = MIX, 32

    def body(g, _):
        at = begin + g * size
        factors = [coef[0, at + b] for b in range(size)]
        for start in range(0, features, chunk):
            part = pl.ds(start, chunk)
            total = acc[part, :]
            for b in range(size):
                total = total + factors[b] * basis[at + b, part, :].astype(f32)
            acc[part, :] = total
        return 0

    lax.fori_loop(0, (end - begin) // size, body, 0, unroll=True)


def send_kernel(n_dst, coef, mask, src, dst, table, weights, basis, _, messages, *rest):
    outs, acc = rest[:n_dst], rest[n_dst]
    count, _, cols = basis.shape
    blocks, block = src.shape[1:]
    per_owner = blocks // n_dst
    span = per_owner * block

    columns = [spread_rows(src[0, k : k + 1, :], block) for k in range(blocks)]
    picks = jnp.concatenate([one_hot(c, table.shape[0]) for c in columns], axis=0)
    picked = jnp.dot(picks, table[...], preferred_element_type=f32).astype(bf16)
    for k in range(blocks):
        scaled = weights[0, k] * mask[0, k].astype(f32).astype(bf16)
        messages[k * block : (k + 1) * block, :] = jnp.dot(
            scaled, picked[k * block : (k + 1) * block, :], preferred_element_type=f32
        ).astype(bf16)

    acc[...] = jnp.zeros_like(acc)
    mix(coef, basis, acc, 0, count)
    weight = acc[...].astype(bf16)
    me = lax.axis_index("dst")
    for d in range(n_dst):
        owner = me ^ d
        mine = messages[pl.ds(pl.multiple_of(owner * span, span), span), :]
        outs[d][:span, :] = jnp.dot(mine, weight, preferred_element_type=f32).astype(bf16)
        pad = outs[d].shape[0] - span
        which = lax.broadcasted_iota(i32, (pad, block), 0)
        slots = jnp.zeros((pad, block), i32)
        for b in range(per_owner):
            ids = dst[0, pl.ds(owner * per_owner + b, 1), :]
            slots = jnp.where(which == 2 * b, ids & 255, slots)
            slots = jnp.where(which == 2 * b + 1, ids >> 8, slots)
        outs[d][span:, :block] = slots.astype(f32).astype(bf16)
        outs[d][span:, block:] = jnp.zeros((pad, cols - block), bf16)


def send(coef, mask, src, dst, table, weights, basis, after, n_dst):
    features, cols = basis.shape[1:]
    blocks, block = src.shape[1:]
    span = blocks // n_dst * block
    pad = -(-2 * (blocks // n_dst) // 16) * 16
    return pl.pallas_call(
        functools.partial(send_kernel, n_dst),
        in_specs=[whole(pltpu.SMEM)] * 2 + [whole()] * 5 + [whole(pl.ANY)],
        out_shape=[jax.ShapeDtypeStruct((blocks * block, features), bf16)]
        + [jax.ShapeDtypeStruct((span + pad, cols), bf16)] * n_dst,
        out_specs=[whole()] * (1 + n_dst),
        scratch_shapes=[pltpu.VMEM((features, cols), f32)],
        compiler_params=pltpu.CompilerParams(vmem_limit_bytes=LIMIT),
        cost_estimate=pl.CostEstimate(flops=6_000_000_000, bytes_accessed=10_000_000, transcendentals=0),
        name="send",
    )(coef, mask, src, dst, table, weights, basis, after)


def first_kernel(out):
    out[...] = jnp.zeros_like(out)


def first():
    return pl.pallas_call(
        first_kernel,
        out_shape=jax.ShapeDtypeStruct((8, 128), f32),
        out_specs=whole(),
        compiler_params=pltpu.CompilerParams(vmem_limit_bytes=LIMIT),
        cost_estimate=pl.CostEstimate(flops=FIRST_FLOPS, bytes_accessed=4096, transcendentals=0),
        name="first",
    )()


def stack_kernel(type_rows, bias, _, *refs):
    parts, out, added = refs[:-2], refs[-2], refs[-1]
    rows_dev, cols = added.shape
    for d, part in enumerate(parts):
        out[d * rows_dev : (d + 1) * rows_dev, :] = part[...]
    row = lax.broadcasted_iota(i32, (rows_dev, cols), 0) + lax.axis_index("rel") * rows_dev
    total = jnp.broadcast_to(bias[0:1, :], (rows_dev, cols))
    bound = 0
    for c in range(bias.shape[0] - 1):
        bound = bound + type_rows[c]
        total = jnp.where(row >= bound, bias[c + 1 : c + 2, :], total)
    added[...] = total


def stack(type_rows, bias, after, parts):
    rows_dev, cols = parts[0].shape
    return pl.pallas_call(
        stack_kernel,
        in_specs=[whole(pltpu.SMEM), whole(), whole(pl.ANY)] + [whole()] * len(parts),
        out_shape=[
            jax.ShapeDtypeStruct((len(parts) * rows_dev, cols), bf16),
            jax.ShapeDtypeStruct((rows_dev, cols), f32),
        ],
        out_specs=[whole()] * 2,
        compiler_params=pltpu.CompilerParams(vmem_limit_bytes=LIMIT),
        name="stack",
    )(type_rows, bias, after, *parts)


def outer_kernel(n_rel, n_dst, near, dst, messages, *rest):
    stacks, outer, late = rest[:near], rest[near], rest[near + 1 :]
    blocks, block = dst.shape[1:]
    rows_dev = stacks[0].shape[0] // n_dst
    span = blocks // n_dst * block
    rel, me = lax.axis_index("rel"), lax.axis_index("dst")
    early = [[] for _ in range(near)]
    for d in range(n_dst):
        owner = me ^ d
        columns = [
            spread_rows(dst[0, pl.ds(owner * (span // block) + b, 1), :], block)
            for b in range(span // block)
        ]
        picks = jnp.concatenate(
            [
                jnp.concatenate(
                    [one_hot(c - (rel ^ e) * rows_dev, rows_dev) for e in range(n_rel)], axis=1
                )
                for c in columns
            ],
            axis=0,
        )
        summed = lax.dot_general(
            messages[pl.ds(pl.multiple_of(owner * span, span), span), :],
            picks,
            CONTRACT_ROWS,
            preferred_element_type=f32,
        ).astype(bf16)
        for e in range(n_rel):
            part = summed[:, e * rows_dev : (e + 1) * rows_dev]
            if e < near:
                early[e].append(part)
            else:
                late[e - near][:, d * rows_dev : (d + 1) * rows_dev] = part
    total = None
    for e in range(near):
        left = jnp.concatenate(early[e], axis=1)
        more = jnp.dot(left, stacks[e][...], preferred_element_type=f32)
        total = more if total is None else total + more
    outer[...] = total


def outer(dst, messages, stacks, n_rel, n_dst):
    features = messages.shape[1]
    rows, cols = stacks[0].shape
    near = len(stacks)
    return pl.pallas_call(
        functools.partial(outer_kernel, n_rel, n_dst, near),
        in_specs=[whole()] * (2 + near),
        out_shape=[jax.ShapeDtypeStruct((features, cols), f32)]
        + [jax.ShapeDtypeStruct((features, rows), bf16)] * (n_rel - near),
        out_specs=[whole()] * (1 + n_rel - near),
        compiler_params=pltpu.CompilerParams(vmem_limit_bytes=LIMIT),
        cost_estimate=pl.CostEstimate(flops=2_000_000_000, bytes_accessed=4_000_000, transcendentals=0),
        name="outer",
    )(dst, messages, *stacks)


def grad_kernel(count_late, basis, partial, *rest):
    lefts, rights = rest[:count_late], rest[count_late : 2 * count_late]
    out, outer, sums = rest[2 * count_late :]
    count, features, cols = basis.shape
    total = partial[...]
    for left, right in zip(lefts, rights):
        total = total + jnp.dot(left[...], right[...], preferred_element_type=f32)
    outer[...] = total

    size = 4

    def contract(g, _):
        totals = [jnp.zeros((8, 128), f32)] * size
        for start in range(0, features, 16):
            part = pl.ds(start, 16)
            side = outer[part, :]
            for b in range(size):
                prod = basis[g * size + b, part, :].astype(f32) * side
                more = prod[:8, :] + prod[8:, :]
                for c in range(0, cols, 128):
                    totals[b] = totals[b] + more[:, c : c + 128]
        for b in range(size):
            sums[pl.ds(g * size + b, 1), :] = jnp.sum(totals[b], axis=0, keepdims=True)
        return 0

    lax.fori_loop(0, count // size, contract, 0)
    out[...] = jnp.sum(sums[...].T, axis=0, keepdims=True)


def grad(basis, partial, lefts, rights):
    features, cols = basis.shape[1:]
    return pl.pallas_call(
        functools.partial(grad_kernel, len(lefts)),
        in_specs=[whole()] * (2 + 2 * len(lefts)),
        out_shape=jax.ShapeDtypeStruct((1, 128), f32),
        out_specs=whole(),
        scratch_shapes=[pltpu.VMEM((features, cols), f32), pltpu.VMEM((128, 128), f32)],
        compiler_params=pltpu.CompilerParams(vmem_limit_bytes=LIMIT),
        cost_estimate=pl.CostEstimate(flops=4_000_000_000, bytes_accessed=10_000_000, transcendentals=0),
        name="grad",
    )(basis, partial, *lefts, *rights)


def gather_kernel(n_rel, n_dst, block, added, *refs):
    got, outs = refs[:n_dst], refs[n_dst:]
    rows_dev = outs[0].shape[0]
    span = got[0].shape[0] // block * block
    rel = lax.axis_index("rel")
    ids = []
    for d in range(n_dst):
        pairs = got[d][span:, :block].astype(f32)
        ids.append(
            [
                (pairs[2 * b : 2 * b + 1] + 256.0 * pairs[2 * b + 1 : 2 * b + 2]).astype(i32)
                for b in range(span // block)
            ]
        )
    row = lax.broadcasted_iota(i32, (rows_dev, block), 0)
    for e in range(n_rel):
        place = row + (rel ^ e) * rows_dev
        total = None
        for d in range(n_dst):
            picks = jnp.concatenate(
                [(place == one).astype(bf16) for one in ids[d]], axis=1
            )
            more = jnp.dot(picks, got[d][:span, :], preferred_element_type=f32)
            total = more if total is None else total + more
        if e == 0:
            total = total + added[...]
        outs[e][...] = total.astype(outs[e].dtype)


def gather(added, got, n_rel, block, rows_dev):
    n_dst, cols = len(got), got[0].shape[1]
    return pl.pallas_call(
        functools.partial(gather_kernel, n_rel, n_dst, block),
        in_specs=[whole()] * (1 + n_dst),
        out_shape=[
            jax.ShapeDtypeStruct((rows_dev, cols), f32 if e == 0 else bf16)
            for e in range(n_rel)
        ],
        out_specs=[whole()] * n_rel,
        compiler_params=pltpu.CompilerParams(vmem_limit_bytes=LIMIT),
        cost_estimate=pl.CostEstimate(flops=600_000_000, bytes_accessed=1_000_000, transcendentals=0),
        name="gather",
    )(added, *got)


def finish_kernel(*refs):
    parts, out = refs[:-1], refs[-1]
    total = parts[0][...]
    for part in parts[1:]:
        total = total + part[...].astype(f32)
    out[...] = total.astype(out.dtype)


def finish(parts):
    return pl.pallas_call(
        finish_kernel,
        in_specs=[whole()] * len(parts),
        out_shape=jax.ShapeDtypeStruct(parts[0].shape, bf16),
        out_specs=whole(),
        compiler_params=pltpu.CompilerParams(vmem_limit_bytes=LIMIT),
        name="finish",
    )(*parts)


def on_device(
    node_table,
    edge_weights,
    src_ids,
    dst_ids,
    block_mask,
    basis_coef,
    basis_mats,
    type_bias,
    type_rows,
    cotangent,
):
    n_rel, n_dst, n_mp = (lax.axis_size(a) for a in ("rel", "dst", "mp"))
    block = edge_weights.shape[-1]
    rows_dev = cotangent.shape[0]

    def swap(x, axis, d):
        n = lax.axis_size(axis)
        return lax.ppermute(x, axis, [(i, i ^ d) for i in range(n)])

    along = [cotangent] + [swap(cotangent, "dst", d) for d in range(1, n_dst)]
    begun = first()
    messages, *queues = send(
        basis_coef,
        block_mask,
        src_ids,
        dst_ids,
        node_table,
        edge_weights,
        basis_mats,
        begun,
        n_dst,
    )
    got = [queues[0]] + [swap(queues[d], "dst", d) for d in range(1, n_dst)]
    stacked, added = stack(type_rows, type_bias, messages, along)

    stacks = [None] * n_rel
    for e in range(0, n_rel, 2):
        stacks[e] = swap(stacked, "rel", e) if e else stacked
        stacks[e + 1] = swap(stacks[e], "rel", 1)
    outer_sum, *lefts = outer(dst_ids, messages, stacks[:2], n_rel, n_dst)
    partial = grad(basis_mats, outer_sum, lefts, stacks[2:])

    sums = gather(added, got, n_rel, block, rows_dev)
    parts = [sums[0]] + [swap(sums[e], "rel", e) for e in range(1, n_rel)]
    layer_out = finish(parts)

    for axis, size in (("mp", n_mp), ("dst", n_dst)):
        d = 1
        while d < size:
            partial = partial + swap(partial, axis, d)
            d *= 2
    return layer_out, partial[:, : basis_coef.shape[1]]


def solution(mesh):
    in_specs = (
        P(("rel", "dst"), None),
        P("rel", "dst", None, None),
        P("rel", "dst", None),
        P("rel", "dst", None),
        P("rel", "dst"),
        P("rel", None),
        P(None, None, "mp"),
        P(None, "mp"),
        P(),
        P(("rel", "dst"), "mp"),
    )
    out_specs = (P(("rel", "dst"), "mp"), P("rel", None))

    return jax.shard_map(
        on_device, mesh=mesh, in_specs=in_specs, out_specs=out_specs, check_vma=False
    )
```

profile of v0, /device:TPU:0, one launch (start us, length us, event | category | flops | bytes accessed | tf_op | source)
XLA Modules:
  0.0 48.3 jit_solution(13876475301430261735)
XLA Ops:
  0.7 3.1 %collective-permute-start = (bf16[128,256]{1,0:T(8,128)(2,1)}, bf16[128,256]{1,0:T(8,128)(2,1)S(1)}, u32[]{:S(2)}, u32[]{:S(2)}) collective-permute-start(bf16[128,256]{1,0:T(8,128)(2,1)} %refs_0_.1), channel_id=1, source_target_pairs={{0,2},{2,0},{4,6},{6,4},{1,3},{3,1},{5,7},{7,5},{8,10},{10,8},{12,... | collective-permute-start | bytes 196616 | tf_op jit(solution)/shard_map/ppermute | solution.py:330
  3.8 2.6 %collective-permute-start.1 = (bf16[128,256]{1,0:T(8,128)(2,1)}, bf16[128,256]{1,0:T(8,128)(2,1)S(1)}, u32[]{:S(2)}, u32[]{:S(2)}) collective-permute-start(bf16[128,256]{1,0:T(8,128)(2,1)} %refs_0_.1), channel_id=1, source_target_pairs={{0,4},{2,6},{4,0},{6,2},{1,5},{3,7},{5,1},{7,3},{8,12},{10,14},{12... | collective-permute-start | bytes 196616 | tf_op jit(solution)/shard_map/ppermute | solution.py:330
  6.5 0.0 copy-start
  6.5 0.0 copy-start.1
  6.5 0.0 copy-start.2
  6.5 4.0 %send.1 = (bf16[1024,512]{1,0:T(8,128)(2,1)S(1)}, bf16[272,256]{1,0:T(8,128)(2,1)S(1)}, bf16[272,256]{1,0:T(8,128)(2,1)S(1)}, bf16[272,256]{1,0:T(8,128)(2,1)S(1)}, bf16[272,256]{1,0:T(8,128)(2,1)S(1)}) custom-call(f32[1,32]{1,0:T(1,128)S(1)} %copy-done.8, s32[1,8]{1,0:T(1,128)S(1)} %copy-done.9, s32[1,8,128]{2,1,0:T(8,128)S(1)} %copy-done.6, ...), custom_call_target="tpu_custom_call" | custom-call | flops 6000000000 | bytes 10000000 | tf_op jit(solution)/shard_map/send/pallas_call | solution.py:90
  10.5 0.0 collective-permute-done.refs_1_
  10.6 0.8 %collective-permute-done.1.refs_2_ = bf16[128,256]{1,0:T(8,128)(2,1)S(1)} collective-permute-done((bf16[128,256]{1,0:T(8,128)(2,1)}, bf16[128,256]{1,0:T(8,128)(2,1)S(1)}, u32[]{:S(2)}, u32[]{:S(2)}) %collective-permute-start.1) | collective-permute-done | bytes 65568 | tf_op jit(solution)/shard_map/ppermute | solution.py:330
  11.3 1.4 %collective-permute-done.2.refs_3_ = bf16[128,256]{1,0:T(8,128)(2,1)S(1)} collective-permute-done((bf16[128,256]{1,0:T(8,128)(2,1)}, bf16[128,256]{1,0:T(8,128)(2,1)S(1)}, u32[]{:S(2)}, u32[]{:S(2)}) %collective-permute-start.2) | collective-permute-done | bytes 65568 | tf_op jit(solution)/shard_map/ppermute | solution.py:330
  12.7 0.6 %stack.1 = (bf16[512,256]{1,0:T(8,128)(2,1)S(1)}, f32[128,256]{1,0:T(8,128)S(1)}) custom-call(s32[4]{0:T(128)S(1)} %copy-done.2, f32[4,256]{1,0:T(4,128)S(1)} %copy-done.1, bf16[1024,512]{1,0:T(8,128)(2,1)S(1)} %get-tuple-element.16._.messages, bf16[128,256]{1,0:T(8,128)(2,1)S(1)} %copy-done, bf16[128,256]{1,0:T(8,128)(2,1)S(1)} %collective-permute-done.refs_1_, ...), custom_call_target="tpu_custom_call" | custom-call | tf_op jit(solution)/shard_map/stack/pallas_call | solution.py:134
  13.3 1.6 %collective-permute-start.10 = (bf16[512,256]{1,0:T(8,128)(2,1)S(1)}, bf16[512,256]{1,0:T(8,128)(2,1)S(1)}, u32[]{:S(2)}, u32[]{:S(2)}) collective-permute-start(bf16[512,256]{1,0:T(8,128)(2,1)S(1)} %get-tuple-element.26.rest_0_), channel_id=1, source_target_pairs={{0,16},{8,24},{16,0},{24,8},{1,17},{9,25},{17,1},{25,9},{2,18},{10... | collective-permute-start | bytes 786440 | tf_op jit(solution)/shard_map/ppermute | solution.py:330
  14.9 0.0 collective-permute-start.9
  14.9 0.0 collective-permute-start.3
  14.9 2.3 %collective-permute-start.4 = (bf16[272,256]{1,0:T(8,128)(2,1)S(1)}, bf16[272,256]{1,0:T(8,128)(2,1)S(1)}, u32[]{:S(2)}, u32[]{:S(2)}) collective-permute-start(bf16[272,256]{1,0:T(8,128)(2,1)S(1)} %get-tuple-element.20), channel_id=1, source_target_pairs={{0,4},{2,6},{4,0},{6,2},{1,5},{3,7},{5,1},{7,3},{8,12},{10,14},{12... | collective-permute-start | bytes 417800 | tf_op jit(solution)/shard_map/ppermute | solution.py:330
  17.2 2.1 %collective-permute-start.5 = (bf16[272,256]{1,0:T(8,128)(2,1)S(1)}, bf16[272,256]{1,0:T(8,128)(2,1)S(1)}, u32[]{:S(2)}, u32[]{:S(2)}) collective-permute-start(bf16[272,256]{1,0:T(8,128)(2,1)S(1)} %get-tuple-element.21), channel_id=1, source_target_pairs={{0,6},{2,4},{4,2},{6,0},{1,7},{3,5},{5,3},{7,1},{8,14},{10,12},{12... | collective-permute-start | bytes 417800 | tf_op jit(solution)/shard_map/ppermute | solution.py:330
  19.3 0.5 %collective-permute-done.10.rest_2_ = bf16[512,256]{1,0:T(8,128)(2,1)S(1)} collective-permute-done((bf16[512,256]{1,0:T(8,128)(2,1)S(1)}, bf16[512,256]{1,0:T(8,128)(2,1)S(1)}, u32[]{:S(2)}, u32[]{:S(2)}) %collective-permute-start.10) | collective-permute-done | bytes 262176 | tf_op jit(solution)/shard_map/ppermute | solution.py:330
  19.8 4.0 %collective-permute-done.3.refs_1_ = bf16[272,256]{1,0:T(8,128)(2,1)S(1)} collective-permute-done((bf16[272,256]{1,0:T(8,128)(2,1)S(1)}, bf16[272,256]{1,0:T(8,128)(2,1)S(1)}, u32[]{:S(2)}, u32[]{:S(2)}) %collective-permute-start.3) | collective-permute-done | bytes 139296 | tf_op jit(solution)/shard_map/ppermute | solution.py:330
  23.8 4.6 %collective-permute-done.4.refs_2_ = bf16[272,256]{1,0:T(8,128)(2,1)S(1)} collective-permute-done((bf16[272,256]{1,0:T(8,128)(2,1)S(1)}, bf16[272,256]{1,0:T(8,128)(2,1)S(1)}, u32[]{:S(2)}, u32[]{:S(2)}) %collective-permute-start.4) | collective-permute-done | bytes 139296 | tf_op jit(solution)/shard_map/ppermute | solution.py:330
  28.3 0.5 gather.1
  28.8 0.1 collective-permute-start.6
  28.9 0.6 %collective-permute-start.7 = (bf16[128,256]{1,0:T(8,128)(2,1)S(1)}, bf16[128,256]{1,0:T(8,128)(2,1)S(1)}, u32[]{:S(2)}, u32[]{:S(2)}) collective-permute-start(bf16[128,256]{1,0:T(8,128)(2,1)S(1)} %get-tuple-element.24), channel_id=1, source_target_pairs={{0,16},{8,24},{16,0},{24,8},{1,17},{9,25},{17,1},{25,9},{2,18},{10... | collective-permute-start | bytes 196616 | tf_op jit(solution)/shard_map/ppermute | solution.py:330
  29.5 1.3 %collective-permute-start.8 = (bf16[128,256]{1,0:T(8,128)(2,1)S(1)}, bf16[128,256]{1,0:T(8,128)(2,1)S(1)}, u32[]{:S(2)}, u32[]{:S(2)}) collective-permute-start(bf16[128,256]{1,0:T(8,128)(2,1)S(1)} %get-tuple-element.25), channel_id=1, source_target_pairs={{0,24},{8,16},{16,8},{24,0},{1,25},{9,17},{17,9},{25,1},{2,26},{10... | collective-permute-start | bytes 196616 | tf_op jit(solution)/shard_map/ppermute | solution.py:330
  30.7 1.2 %outer.1 = (f32[512,256]{1,0:T(8,128)S(1)}, bf16[512,512]{1,0:T(8,128)(2,1)S(1)}, bf16[512,512]{1,0:T(8,128)(2,1)S(1)}) custom-call(s32[1,8,128]{2,1,0:T(8,128)S(1)} %copy-done.7, bf16[1024,512]{1,0:T(8,128)(2,1)S(1)} %get-tuple-element.16._.messages, bf16[512,256]{1,0:T(8,128)(2,1)S(1)} %get-tuple-element.26.rest_0_, ...), custom_call_target="tpu_custom_call" | custom-call | flops 2000000000 | bytes 4000000 | tf_op jit(solution)/shard_map/outer/pallas_call | solution.py:193
  32.0 2.7 %grad.1 = f32[1,128]{1,0:T(1,128)S(1)} custom-call(bf16[32,512,256]{2,1,0:T(8,128)(2,1)S(1)} %copy-done.3, f32[512,256]{1,0:T(8,128)S(1)} %get-tuple-element.27.partial, bf16[512,512]{1,0:T(8,128)(2,1)S(1)} %get-tuple-element.28.rest_0_, bf16[512,512]{1,0:T(8,128)(2,1)S(1)} %get-tuple-element.29.rest_1_, ...), custom_call_target="tpu_custom_call" | custom-call | flops 4000000000 | bytes 10000000 | tf_op jit(solution)/shard_map/grad/pallas_call | solution.py:236
  34.7 1.6 %collective-permute-start.12 = (f32[1,128]{1,0:T(1,128)S(1)}, f32[1,128]{1,0:T(1,128)S(1)}, u32[]{:S(2)}, u32[]{:S(2)}) collective-permute-start(f32[1,128]{1,0:T(1,128)S(1)} %grad.1), channel_id=1, source_target_pairs={{0,1},{1,0},{2,3},{3,2},{4,5},{5,4},{6,7},{7,6},{8,9},{9,8},{10,11... | collective-permute-start | bytes 1544 | tf_op jit(solution)/shard_map/ppermute | solution.py:330
  36.3 2.0 %collective-permute-done.12 = f32[1,128]{1,0:T(1,128)S(1)} collective-permute-done((f32[1,128]{1,0:T(1,128)S(1)}, f32[1,128]{1,0:T(1,128)S(1)}, u32[]{:S(2)}, u32[]{:S(2)}) %collective-permute-start.12) | collective-permute-done | bytes 544 | tf_op jit(solution)/shard_map/ppermute | solution.py:330
  38.3 3.1 %collective-permute-start.13 = (f32[1,128]{1,0:T(1,128)S(1)}, f32[1,128]{1,0:T(1,128)S(1)}, u32[]{:S(2)}, u32[]{:S(2)}) collective-permute-start(f32[1,128]{1,0:T(1,128)S(1)} %add.9), channel_id=1, source_target_pairs={{0,2},{2,0},{4,6},{6,4},{1,3},{3,1},{5,7},{7,5},{8,10},{10,8},{12,... | collective-permute-start | bytes 1544 | tf_op jit(solution)/shard_map/ppermute | solution.py:330
  41.4 1.5 %collective-permute-done.13 = f32[1,128]{1,0:T(1,128)S(1)} collective-permute-done((f32[1,128]{1,0:T(1,128)S(1)}, f32[1,128]{1,0:T(1,128)S(1)}, u32[]{:S(2)}, u32[]{:S(2)}) %collective-permute-start.13) | collective-permute-done | bytes 544 | tf_op jit(solution)/shard_map/ppermute | solution.py:330
  43.0 3.3 %collective-permute-start.14 = (f32[1,128]{1,0:T(1,128)S(1)}, f32[1,128]{1,0:T(1,128)S(1)}, u32[]{:S(2)}, u32[]{:S(2)}) collective-permute-start(f32[1,128]{1,0:T(1,128)S(1)} %add.10), channel_id=1, source_target_pairs={{0,4},{2,6},{4,0},{6,2},{1,5},{3,7},{5,1},{7,3},{8,12},{10,14},{12... | collective-permute-start | bytes 1544 | tf_op jit(solution)/shard_map/ppermute | solution.py:330
  46.3 0.7 %finish.1 = bf16[128,256]{1,0:T(8,128)(2,1)} custom-call(f32[128,256]{1,0:T(8,128)S(1)} %get-tuple-element.22.refs_0_, bf16[128,256]{1,0:T(8,128)(2,1)S(1)} %collective-permute-done.6.refs_1_, bf16[128,256]{1,0:T(8,128)(2,1)S(1)} %collective-permute-done.7.refs_2_, bf16[128,256]{1,0:T(8,128)(2,1)S(1)} %collective-permute-done.8.refs_3_), custom_call_target="tpu_custom_call" | custom-call | tf_op jit(solution)/shard_map/finish/pallas_call | solution.py:302
  47.0 0.9 %collective-permute-done.14 = f32[1,128]{1,0:T(1,128)S(1)} collective-permute-done((f32[1,128]{1,0:T(1,128)S(1)}, f32[1,128]{1,0:T(1,128)S(1)}, u32[]{:S(2)}, u32[]{:S(2)}) %collective-permute-start.14) | collective-permute-done | bytes 544 | tf_op jit(solution)/shard_map/ppermute | solution.py:330
  47.8 0.5 %add.11 = f32[1,128]{1,0:T(1,128)} add(f32[1,128]{1,0:T(1,128)S(1)} %add.10, f32[1,128]{1,0:T(1,128)S(1)} %collective-permute-done.14) | non-fusion elementwise | flops 128 | bytes 1536 | tf_op jit(solution)/shard_map/add | solution.py:362
  (28 shorter events, 0.1 us)
Async XLA Ops:
  0.6 5.8 %copy-start.8 = (f32[1,32]{1,0:T(1,128)S(1)}, f32[1,32]{1,0:T(1,128)}, u32[]{:S(2)}) copy-start(f32[1,32]{1,0:T(1,128)} %coef.1) | copy-start | bytes 388
  0.6 5.8 %copy-start.9 = (s32[1,8]{1,0:T(1,128)S(1)}, s32[1,8]{1,0:T(1,128)}, u32[]{:S(2)}) copy-start(s32[1,8]{1,0:T(1,128)} %mask.1) | copy-start | bytes 100
  0.7 5.8 %copy-start.6 = (s32[1,8,128]{2,1,0:T(8,128)S(1)}, s32[1,8,128]{2,1,0:T(8,128)}, u32[]{:S(2)}) copy-start(s32[1,8,128]{2,1,0:T(8,128)} %src.1) | copy-start | bytes 12292
  0.7 5.8 %copy-start.7 = (s32[1,8,128]{2,1,0:T(8,128)S(1)}, s32[1,8,128]{2,1,0:T(8,128)}, u32[]{:S(2)}) copy-start(s32[1,8,128]{2,1,0:T(8,128)} %dst.3) | copy-start | bytes 12292
  0.7 5.8 %copy-start.4 = (bf16[1024,512]{1,0:T(8,128)(2,1)S(1)}, bf16[1024,512]{1,0:T(8,128)(2,1)}, u32[]{:S(2)}) copy-start(bf16[1024,512]{1,0:T(8,128)(2,1)} %table.1) | copy-start | bytes 3145732
  0.7 5.8 %copy-start.5 = (bf16[1,8,128,128]{3,2,1,0:T(8,128)(2,1)S(1)}, bf16[1,8,128,128]{3,2,1,0:T(8,128)(2,1)}, u32[]{:S(2)}) copy-start(bf16[1,8,128,128]{3,2,1,0:T(8,128)(2,1)} %weights.1) | copy-start | bytes 786436
  0.7 5.8 %copy-start.3 = (bf16[32,512,256]{2,1,0:T(8,128)(2,1)S(1)}, bf16[32,512,256]{2,1,0:T(8,128)(2,1)}, u32[]{:S(2)}) copy-start(bf16[32,512,256]{2,1,0:T(8,128)(2,1)} %basis.3) | copy-start | bytes 25165828
  0.7 9.8 %collective-permute-start = (bf16[128,256]{1,0:T(8,128)(2,1)}, bf16[128,256]{1,0:T(8,128)(2,1)S(1)}, u32[]{:S(2)}, u32[]{:S(2)}) collective-permute-start(bf16[128,256]{1,0:T(8,128)(2,1)} %refs_0_.1), channel_id=1, source_target_pairs={{0,2},{2,0},{4,6},{6,4},{1,3},{3,1},{5,7},{7,5},{8,10},{10,8},{12,... | collective-permute-start | bytes 196616 | tf_op jit(solution)/shard_map/ppermute | solution.py:330
  3.8 7.5 %collective-permute-start.1 = (bf16[128,256]{1,0:T(8,128)(2,1)}, bf16[128,256]{1,0:T(8,128)(2,1)S(1)}, u32[]{:S(2)}, u32[]{:S(2)}) collective-permute-start(bf16[128,256]{1,0:T(8,128)(2,1)} %refs_0_.1), channel_id=1, source_target_pairs={{0,4},{2,6},{4,0},{6,2},{1,5},{3,7},{5,1},{7,3},{8,12},{10,14},{12... | collective-permute-start | bytes 196616 | tf_op jit(solution)/shard_map/ppermute | solution.py:330
  6.4 6.3 %collective-permute-start.2 = (bf16[128,256]{1,0:T(8,128)(2,1)}, bf16[128,256]{1,0:T(8,128)(2,1)S(1)}, u32[]{:S(2)}, u32[]{:S(2)}) collective-permute-start(bf16[128,256]{1,0:T(8,128)(2,1)} %refs_0_.1), channel_id=1, source_target_pairs={{0,6},{2,4},{4,2},{6,0},{1,7},{3,5},{5,3},{7,1},{8,14},{10,12},{12... | collective-permute-start | bytes 196616 | tf_op jit(solution)/shard_map/ppermute | solution.py:330
  6.5 6.2 %copy-start = (bf16[128,256]{1,0:T(8,128)(2,1)S(1)}, bf16[128,256]{1,0:T(8,128)(2,1)}, u32[]{:S(2)}) copy-start(bf16[128,256]{1,0:T(8,128)(2,1)} %refs_0_.1) | copy-start | bytes 196612
  6.5 6.2 %copy-start.1 = (f32[4,256]{1,0:T(4,128)S(1)}, f32[4,256]{1,0:T(4,128)}, u32[]{:S(2)}) copy-start(f32[4,256]{1,0:T(4,128)} %bias.1) | copy-start | bytes 12292
  6.5 6.2 %copy-start.2 = (s32[4]{0:T(128)S(1)}, s32[4]{0:T(128)}, u32[]{:S(2)}) copy-start(s32[4]{0:T(128)} %type_rows.1) | copy-start | bytes 52
  13.3 6.5 %collective-permute-start.10 = (bf16[512,256]{1,0:T(8,128)(2,1)S(1)}, bf16[512,256]{1,0:T(8,128)(2,1)S(1)}, u32[]{:S(2)}, u32[]{:S(2)}) collective-permute-start(bf16[512,256]{1,0:T(8,128)(2,1)S(1)} %get-tuple-element.26.rest_0_), channel_id=1, source_target_pairs={{0,16},{8,24},{16,0},{24,8},{1,17},{9,25},{17,1},{25,9},{2,18},{10... | collective-permute-start | bytes 786440 | tf_op jit(solution)/shard_map/ppermute | solution.py:330
  14.9 15.9 %collective-permute-start.9 = (bf16[512,256]{1,0:T(8,128)(2,1)S(1)}, bf16[512,256]{1,0:T(8,128)(2,1)S(1)}, u32[]{:S(2)}, u32[]{:S(2)}) collective-permute-start(bf16[512,256]{1,0:T(8,128)(2,1)S(1)} %get-tuple-element.26.rest_0_), channel_id=1, source_target_pairs={{0,8},{8,0},{16,24},{24,16},{1,9},{9,1},{17,25},{25,17},{2,10},{10... | collective-permute-start | bytes 786440 | tf_op jit(solution)/shard_map/ppermute | solution.py:330
  14.9 8.9 %collective-permute-start.3 = (bf16[272,256]{1,0:T(8,128)(2,1)S(1)}, bf16[272,256]{1,0:T(8,128)(2,1)S(1)}, u32[]{:S(2)}, u32[]{:S(2)}) collective-permute-start(bf16[272,256]{1,0:T(8,128)(2,1)S(1)} %get-tuple-element.19), channel_id=1, source_target_pairs={{0,2},{2,0},{4,6},{6,4},{1,3},{3,1},{5,7},{7,5},{8,10},{10,8},{12,... | collective-permute-start | bytes 417800 | tf_op jit(solution)/shard_map/ppermute | solution.py:330
  14.9 13.5 %collective-permute-start.4 = (bf16[272,256]{1,0:T(8,128)(2,1)S(1)}, bf16[272,256]{1,0:T(8,128)(2,1)S(1)}, u32[]{:S(2)}, u32[]{:S(2)}) collective-permute-start(bf16[272,256]{1,0:T(8,128)(2,1)S(1)} %get-tuple-element.20), channel_id=1, source_target_pairs={{0,4},{2,6},{4,0},{6,2},{1,5},{3,7},{5,1},{7,3},{8,12},{10,14},{12... | collective-permute-start | bytes 417800 | tf_op jit(solution)/shard_map/ppermute | solution.py:330
  17.2 11.1 %collective-permute-start.5 = (bf16[272,256]{1,0:T(8,128)(2,1)S(1)}, bf16[272,256]{1,0:T(8,128)(2,1)S(1)}, u32[]{:S(2)}, u32[]{:S(2)}) collective-permute-start(bf16[272,256]{1,0:T(8,128)(2,1)S(1)} %get-tuple-element.21), channel_id=1, source_target_pairs={{0,6},{2,4},{4,2},{6,0},{1,7},{3,5},{5,3},{7,1},{8,14},{10,12},{12... | collective-permute-start | bytes 417800 | tf_op jit(solution)/shard_map/ppermute | solution.py:330
  19.8 12.2 %collective-permute-start.11 = (bf16[512,256]{1,0:T(8,128)(2,1)S(1)}, bf16[512,256]{1,0:T(8,128)(2,1)S(1)}, u32[]{:S(2)}, u32[]{:S(2)}) collective-permute-start(bf16[512,256]{1,0:T(8,128)(2,1)S(1)} %collective-permute-done.10.rest_2_), channel_id=1, source_target_pairs={{0,8},{8,0},{16,24},{24,16},{1,9},{9,1},{17,25},{25,17},{2,10},{10... | collective-permute-start | bytes 786440 | tf_op jit(solution)/shard_map/ppermute | solution.py:330
  28.8 17.5 %collective-permute-start.6 = (bf16[128,256]{1,0:T(8,128)(2,1)S(1)}, bf16[128,256]{1,0:T(8,128)(2,1)S(1)}, u32[]{:S(2)}, u32[]{:S(2)}) collective-permute-start(bf16[128,256]{1,0:T(8,128)(2,1)S(1)} %get-tuple-element.23), channel_id=1, source_target_pairs={{0,8},{8,0},{16,24},{24,16},{1,9},{9,1},{17,25},{25,17},{2,10},{10... | collective-permute-start | bytes 196616 | tf_op jit(solution)/shard_map/ppermute | solution.py:330
  28.9 17.4 %collective-permute-start.7 = (bf16[128,256]{1,0:T(8,128)(2,1)S(1)}, bf16[128,256]{1,0:T(8,128)(2,1)S(1)}, u32[]{:S(2)}, u32[]{:S(2)}) collective-permute-start(bf16[128,256]{1,0:T(8,128)(2,1)S(1)} %get-tuple-element.24), channel_id=1, source_target_pairs={{0,16},{8,24},{16,0},{24,8},{1,17},{9,25},{17,1},{25,9},{2,18},{10... | collective-permute-start | bytes 196616 | tf_op jit(solution)/shard_map/ppermute | solution.py:330
  29.5 16.8 %collective-permute-start.8 = (bf16[128,256]{1,0:T(8,128)(2,1)S(1)}, bf16[128,256]{1,0:T(8,128)(2,1)S(1)}, u32[]{:S(2)}, u32[]{:S(2)}) collective-permute-start(bf16[128,256]{1,0:T(8,128)(2,1)S(1)} %get-tuple-element.25), channel_id=1, source_target_pairs={{0,24},{8,16},{16,8},{24,0},{1,25},{9,17},{17,9},{25,1},{2,26},{10... | collective-permute-start | bytes 196616 | tf_op jit(solution)/shard_map/ppermute | solution.py:330
  34.7 3.6 %collective-permute-start.12 = (f32[1,128]{1,0:T(1,128)S(1)}, f32[1,128]{1,0:T(1,128)S(1)}, u32[]{:S(2)}, u32[]{:S(2)}) collective-permute-start(f32[1,128]{1,0:T(1,128)S(1)} %grad.1), channel_id=1, source_target_pairs={{0,1},{1,0},{2,3},{3,2},{4,5},{5,4},{6,7},{7,6},{8,9},{9,8},{10,11... | collective-permute-start | bytes 1544 | tf_op jit(solution)/shard_map/ppermute | solution.py:330
  38.3 4.6 %collective-permute-start.13 = (f32[1,128]{1,0:T(1,128)S(1)}, f32[1,128]{1,0:T(1,128)S(1)}, u32[]{:S(2)}, u32[]{:S(2)}) collective-permute-start(f32[1,128]{1,0:T(1,128)S(1)} %add.9), channel_id=1, source_target_pairs={{0,2},{2,0},{4,6},{6,4},{1,3},{3,1},{5,7},{7,5},{8,10},{10,8},{12,... | collective-permute-start | bytes 1544 | tf_op jit(solution)/shard_map/ppermute | solution.py:330
  43.0 4.8 %collective-permute-start.14 = (f32[1,128]{1,0:T(1,128)S(1)}, f32[1,128]{1,0:T(1,128)S(1)}, u32[]{:S(2)}, u32[]{:S(2)}) collective-permute-start(f32[1,128]{1,0:T(1,128)S(1)} %add.10), channel_id=1, source_target_pairs={{0,4},{2,6},{4,0},{6,2},{1,5},{3,7},{5,1},{7,3},{8,12},{10,14},{12... | collective-permute-start | bytes 1544 | tf_op jit(solution)/shard_map/ppermute | solution.py:330
where the time goes:
time: 48.5 us; the launch traced here: 48.3 us
  starting transfers between devices  21.6 us (45%)
  waiting for transfers between devices  15.7 us (32%)
  Pallas kernels  9.69 us (20%)
  between operations  0.83 us (2%)
  other arithmetic  0.52 us (1%)
    ppermute x15, starting transfers between devices, swap(): return lax.ppermute(x, axis, [(i, i ^ d) for i in range(n)])  21.6 us
    ppermute x15, waiting for transfers between devices, swap(): return lax.ppermute(x, axis, [(i, i ^ d) for i in range(n)])  15.7 us
    pallas_call x1, Pallas kernels, send(): pl.pallas_call(functools.partial(send_kernel, n_dst), in_specs=[whole(plt...  4.03 us
    pallas_call x1, Pallas kernels, grad(): pl.pallas_call(functools.partial(grad_kernel, len(lefts)), in_specs=[whol...  2.7 us
    pallas_call x1, Pallas kernels, outer(): pl.pallas_call(functools.partial(outer_kernel, n_rel, n_dst, near), in_sp...  1.25 us
  transfers between devices with their start and end apart: 15, of which 8 were waited for; matrix products, arithmetic and copies ran while one was open for 0% of the time, Pallas kernels for 11%

commit v1 on v0

--- a/solution.py
+++ b/solution.py
@@ -209,25 +209,26 @@
     total = partial[...]
     for left, right in zip(lefts, rights):
         total = total + jnp.dot(left[...], right[...], preferred_element_type=f32)
-    outer[...] = total
+    outer[...] = total.astype(bf16)
 
     size = 4
 
     def contract(g, _):
         totals = [jnp.zeros((8, 128), f32)] * size
-        for start in range(0, features, 16):
-            part = pl.ds(start, 16)
+        for start in range(0, features, 32):
+            part = pl.ds(start, 32)
             side = outer[part, :]
             for b in range(size):
-                prod = basis[g * size + b, part, :].astype(f32) * side
-                more = prod[:8, :] + prod[8:, :]
-                for c in range(0, cols, 128):
-                    totals[b] = totals[b] + more[:, c : c + 128]
+                prod = basis[g * size + b, part, :] * side
+                more = (prod[:16, :] + prod[16:, :]).astype(f32)
+                for r in range(0, 16, 8):
+                    for c in range(0, cols, 128):
+                        totals[b] = totals[b] + more[r : r + 8, c : c + 128]
         for b in range(size):
             sums[pl.ds(g * size + b, 1), :] = jnp.sum(totals[b], axis=0, keepdims=True)
         return 0
 
-    lax.fori_loop(0, count // size, contract, 0)
+    lax.fori_loop(0, count // size, contract, 0, unroll=True)
     out[...] = jnp.sum(sums[...].T, axis=0, keepdims=True)
 
 
@@ -238,7 +239,7 @@
         in_specs=[whole()] * (2 + 2 * len(lefts)),
         out_shape=jax.ShapeDtypeStruct((1, 128), f32),
         out_specs=whole(),
-        scratch_shapes=[pltpu.VMEM((features, cols), f32), pltpu.VMEM((128, 128), f32)],
+        scratch_shapes=[pltpu.VMEM((features, cols), bf16), pltpu.VMEM((128, 128), f32)],
         compiler_params=pltpu.CompilerParams(vmem_limit_bytes=LIMIT),
         cost_estimate=pl.CostEstimate(flops=4_000_000_000, bytes_accessed=10_000_000, transcendentals=0),
         name="grad",

time: 48.5 us -> 47.2 us (0.973)
  Pallas kernels: 9.69 us -> 8.44 us
    pallas_call x1, Pallas kernels: 2.7 us -> 1.45 us  [grad(): pl.pallas_call(functools.partial(grad_kernel, len(lefts)), in_specs=[whol...]
  transfers between devices with their start and end apart: 15 -> 15, of which waited for: 8 -> 8; matrix products, arithmetic and copies ran while one was open for 0% -> 0% of each run, Pallas kernels for 11% -> 8%
where the time goes in v1:
time: 47.2 us; the launch traced here: 47.1 us
  starting transfers between devices  21.6 us (46%)
  waiting for transfers between devices  15.7 us (33%)
  Pallas kernels  8.44 us (18%)
  between operations  0.83 us (2%)
  other arithmetic  0.52 us (1%)
    ppermute x15, starting transfers between devices, swap(): return lax.ppermute(x, axis, [(i, i ^ d) for i in range(n)])  21.6 us
    ppermute x15, waiting for transfers between devices, swap(): return lax.ppermute(x, axis, [(i, i ^ d) for i in range(n)])  15.7 us
    pallas_call x1, Pallas kernels, send(): pl.pallas_call(functools.partial(send_kernel, n_dst), in_specs=[whole(plt...  4.03 us
    pallas_call x1, Pallas kernels, grad(): pl.pallas_call(functools.partial(grad_kernel, len(lefts)), in_specs=[whol...  1.45 us
    pallas_call x1, Pallas kernels, outer(): pl.pallas_call(functools.partial(outer_kernel, n_rel, n_dst, near), in_sp...  1.25 us
  transfers between devices with their start and end apart: 15, of which 8 were waited for; matrix products, arithmetic and copies ran while one was open for 0% of the time, Pallas kernels for 8%

profile of v1, /device:TPU:0, one launch (start us, length us, event | category | flops | bytes accessed | tf_op | source)
XLA Modules:
  0.0 47.1 jit_solution(12379565943926541220)
XLA Ops:
  0.7 3.1 %collective-permute-start = (bf16[128,256]{1,0:T(8,128)(2,1)}, bf16[128,256]{1,0:T(8,128)(2,1)S(1)}, u32[]{:S(2)}, u32[]{:S(2)}) collective-permute-start(bf16[128,256]{1,0:T(8,128)(2,1)} %refs_0_.1), channel_id=1, source_target_pairs={{0,2},{2,0},{4,6},{6,4},{1,3},{3,1},{5,7},{7,5},{8,10},{10,8},{12,... | collective-permute-start | bytes 196616 | tf_op jit(solution)/shard_map/ppermute | solution.py:331
  3.8 2.6 %collective-permute-start.1 = (bf16[128,256]{1,0:T(8,128)(2,1)}, bf16[128,256]{1,0:T(8,128)(2,1)S(1)}, u32[]{:S(2)}, u32[]{:S(2)}) collective-permute-start(bf16[128,256]{1,0:T(8,128)(2,1)} %refs_0_.1), channel_id=1, source_target_pairs={{0,4},{2,6},{4,0},{6,2},{1,5},{3,7},{5,1},{7,3},{8,12},{10,14},{12... | collective-permute-start | bytes 196616 | tf_op jit(solution)/shard_map/ppermute | solution.py:331
  6.5 0.0 copy-start
  6.5 0.0 copy-start.1
  6.5 0.0 copy-start.2
  6.5 4.0 %send.1 = (bf16[1024,512]{1,0:T(8,128)(2,1)S(1)}, bf16[272,256]{1,0:T(8,128)(2,1)S(1)}, bf16[272,256]{1,0:T(8,128)(2,1)S(1)}, bf16[272,256]{1,0:T(8,128)(2,1)S(1)}, bf16[272,256]{1,0:T(8,128)(2,1)S(1)}) custom-call(f32[1,32]{1,0:T(1,128)S(1)} %copy-done.8, s32[1,8]{1,0:T(1,128)S(1)} %copy-done.9, s32[1,8,128]{2,1,0:T(8,128)S(1)} %copy-done.6, ...), custom_call_target="tpu_custom_call" | custom-call | flops 6000000000 | bytes 10000000 | tf_op jit(solution)/shard_map/send/pallas_call | solution.py:90
  10.5 0.0 collective-permute-done.refs_1_
  10.6 0.8 %collective-permute-done.1.refs_2_ = bf16[128,256]{1,0:T(8,128)(2,1)S(1)} collective-permute-done((bf16[128,256]{1,0:T(8,128)(2,1)}, bf16[128,256]{1,0:T(8,128)(2,1)S(1)}, u32[]{:S(2)}, u32[]{:S(2)}) %collective-permute-start.1) | collective-permute-done | bytes 65568 | tf_op jit(solution)/shard_map/ppermute | solution.py:331
  11.3 1.4 %collective-permute-done.2.refs_3_ = bf16[128,256]{1,0:T(8,128)(2,1)S(1)} collective-permute-done((bf16[128,256]{1,0:T(8,128)(2,1)}, bf16[128,256]{1,0:T(8,128)(2,1)S(1)}, u32[]{:S(2)}, u32[]{:S(2)}) %collective-permute-start.2) | collective-permute-done | bytes 65568 | tf_op jit(solution)/shard_map/ppermute | solution.py:331
  12.7 0.6 %stack.1 = (bf16[512,256]{1,0:T(8,128)(2,1)S(1)}, f32[128,256]{1,0:T(8,128)S(1)}) custom-call(s32[4]{0:T(128)S(1)} %copy-done.2, f32[4,256]{1,0:T(4,128)S(1)} %copy-done.1, bf16[1024,512]{1,0:T(8,128)(2,1)S(1)} %get-tuple-element.16._.messages, bf16[128,256]{1,0:T(8,128)(2,1)S(1)} %copy-done, bf16[128,256]{1,0:T(8,128)(2,1)S(1)} %collective-permute-done.refs_1_, ...), custom_call_target="tpu_custom_call" | custom-call | tf_op jit(solution)/shard_map/stack/pallas_call | solution.py:134
  13.3 1.6 %collective-permute-start.10 = (bf16[512,256]{1,0:T(8,128)(2,1)S(1)}, bf16[512,256]{1,0:T(8,128)(2,1)S(1)}, u32[]{:S(2)}, u32[]{:S(2)}) collective-permute-start(bf16[512,256]{1,0:T(8,128)(2,1)S(1)} %get-tuple-element.26.rest_0_), channel_id=1, source_target_pairs={{0,16},{8,24},{16,0},{24,8},{1,17},{9,25},{17,1},{25,9},{2,18},{10... | collective-permute-start | bytes 786440 | tf_op jit(solution)/shard_map/ppermute | solution.py:331
  14.9 0.0 collective-permute-start.9
  14.9 0.0 collective-permute-start.3
  14.9 2.3 %collective-permute-start.4 = (bf16[272,256]{1,0:T(8,128)(2,1)S(1)}, bf16[272,256]{1,0:T(8,128)(2,1)S(1)}, u32[]{:S(2)}, u32[]{:S(2)}) collective-permute-start(bf16[272,256]{1,0:T(8,128)(2,1)S(1)} %get-tuple-element.20), channel_id=1, source_target_pairs={{0,4},{2,6},{4,0},{6,2},{1,5},{3,7},{5,1},{7,3},{8,12},{10,14},{12... | collective-permute-start | bytes 417800 | tf_op jit(solution)/shard_map/ppermute | solution.py:331
  17.2 2.1 %collective-permute-start.5 = (bf16[272,256]{1,0:T(8,128)(2,1)S(1)}, bf16[272,256]{1,0:T(8,128)(2,1)S(1)}, u32[]{:S(2)}, u32[]{:S(2)}) collective-permute-start(bf16[272,256]{1,0:T(8,128)(2,1)S(1)} %get-tuple-element.21), channel_id=1, source_target_pairs={{0,6},{2,4},{4,2},{6,0},{1,7},{3,5},{5,3},{7,1},{8,14},{10,12},{12... | collective-permute-start | bytes 417800 | tf_op jit(solution)/shard_map/ppermute | solution.py:331
  19.3 0.5 %collective-permute-done.10.rest_2_ = bf16[512,256]{1,0:T(8,128)(2,1)S(1)} collective-permute-done((bf16[512,256]{1,0:T(8,128)(2,1)S(1)}, bf16[512,256]{1,0:T(8,128)(2,1)S(1)}, u32[]{:S(2)}, u32[]{:S(2)}) %collective-permute-start.10) | collective-permute-done | bytes 262176 | tf_op jit(solution)/shard_map/ppermute | solution.py:331
  19.8 4.0 %collective-permute-done.3.refs_1_ = bf16[272,256]{1,0:T(8,128)(2,1)S(1)} collective-permute-done((bf16[272,256]{1,0:T(8,128)(2,1)S(1)}, bf16[272,256]{1,0:T(8,128)(2,1)S(1)}, u32[]{:S(2)}, u32[]{:S(2)}) %collective-permute-start.3) | collective-permute-done | bytes 139296 | tf_op jit(solution)/shard_map/ppermute | solution.py:331
  23.8 4.6 %collective-permute-done.4.refs_2_ = bf16[272,256]{1,0:T(8,128)(2,1)S(1)} collective-permute-done((bf16[272,256]{1,0:T(8,128)(2,1)S(1)}, bf16[272,256]{1,0:T(8,128)(2,1)S(1)}, u32[]{:S(2)}, u32[]{:S(2)}) %collective-permute-start.4) | collective-permute-done | bytes 139296 | tf_op jit(solution)/shard_map/ppermute | solution.py:331
  28.3 0.5 gather.1
  28.8 0.1 collective-permute-start.6
  28.9 0.6 %collective-permute-start.7 = (bf16[128,256]{1,0:T(8,128)(2,1)S(1)}, bf16[128,256]{1,0:T(8,128)(2,1)S(1)}, u32[]{:S(2)}, u32[]{:S(2)}) collective-permute-start(bf16[128,256]{1,0:T(8,128)(2,1)S(1)} %get-tuple-element.24), channel_id=1, source_target_pairs={{0,16},{8,24},{16,0},{24,8},{1,17},{9,25},{17,1},{25,9},{2,18},{10... | collective-permute-start | bytes 196616 | tf_op jit(solution)/shard_map/ppermute | solution.py:331
  29.5 1.3 %collective-permute-start.8 = (bf16[128,256]{1,0:T(8,128)(2,1)S(1)}, bf16[128,256]{1,0:T(8,128)(2,1)S(1)}, u32[]{:S(2)}, u32[]{:S(2)}) collective-permute-start(bf16[128,256]{1,0:T(8,128)(2,1)S(1)} %get-tuple-element.25), channel_id=1, source_target_pairs={{0,24},{8,16},{16,8},{24,0},{1,25},{9,17},{17,9},{25,1},{2,26},{10... | collective-permute-start | bytes 196616 | tf_op jit(solution)/shard_map/ppermute | solution.py:331
  30.7 1.2 %outer.1 = (f32[512,256]{1,0:T(8,128)S(1)}, bf16[512,512]{1,0:T(8,128)(2,1)S(1)}, bf16[512,512]{1,0:T(8,128)(2,1)S(1)}) custom-call(s32[1,8,128]{2,1,0:T(8,128)S(1)} %copy-done.7, bf16[1024,512]{1,0:T(8,128)(2,1)S(1)} %get-tuple-element.16._.messages, bf16[512,256]{1,0:T(8,128)(2,1)S(1)} %get-tuple-element.26.rest_0_, ...), custom_call_target="tpu_custom_call" | custom-call | flops 2000000000 | bytes 4000000 | tf_op jit(solution)/shard_map/outer/pallas_call | solution.py:193
  32.0 1.5 %grad.1 = f32[1,128]{1,0:T(1,128)S(1)} custom-call(bf16[32,512,256]{2,1,0:T(8,128)(2,1)S(1)} %copy-done.3, f32[512,256]{1,0:T(8,128)S(1)} %get-tuple-element.27.partial, bf16[512,512]{1,0:T(8,128)(2,1)S(1)} %get-tuple-element.28.rest_0_, bf16[512,512]{1,0:T(8,128)(2,1)S(1)} %get-tuple-element.29.rest_1_, ...), custom_call_target="tpu_custom_call" | custom-call | flops 4000000000 | bytes 10000000 | tf_op jit(solution)/shard_map/grad/pallas_call | solution.py:237
  33.5 1.6 %collective-permute-start.12 = (f32[1,128]{1,0:T(1,128)S(1)}, f32[1,128]{1,0:T(1,128)S(1)}, u32[]{:S(2)}, u32[]{:S(2)}) collective-permute-start(f32[1,128]{1,0:T(1,128)S(1)} %grad.1), channel_id=1, source_target_pairs={{0,1},{1,0},{2,3},{3,2},{4,5},{5,4},{6,7},{7,6},{8,9},{9,8},{10,11... | collective-permute-start | bytes 1544 | tf_op jit(solution)/shard_map/ppermute | solution.py:331
  35.1 2.0 %collective-permute-done.12 = f32[1,128]{1,0:T(1,128)S(1)} collective-permute-done((f32[1,128]{1,0:T(1,128)S(1)}, f32[1,128]{1,0:T(1,128)S(1)}, u32[]{:S(2)}, u32[]{:S(2)}) %collective-permute-start.12) | collective-permute-done | bytes 544 | tf_op jit(solution)/shard_map/ppermute | solution.py:331
  37.1 3.1 %collective-permute-start.13 = (f32[1,128]{1,0:T(1,128)S(1)}, f32[1,128]{1,0:T(1,128)S(1)}, u32[]{:S(2)}, u32[]{:S(2)}) collective-permute-start(f32[1,128]{1,0:T(1,128)S(1)} %add.9), channel_id=1, source_target_pairs={{0,2},{2,0},{4,6},{6,4},{1,3},{3,1},{5,7},{7,5},{8,10},{10,8},{12,... | collective-permute-start | bytes 1544 | tf_op jit(solution)/shard_map/ppermute | solution.py:331
  40.2 1.5 %collective-permute-done.13 = f32[1,128]{1,0:T(1,128)S(1)} collective-permute-done((f32[1,128]{1,0:T(1,128)S(1)}, f32[1,128]{1,0:T(1,128)S(1)}, u32[]{:S(2)}, u32[]{:S(2)}) %collective-permute-start.13) | collective-permute-done | bytes 544 | tf_op jit(solution)/shard_map/ppermute | solution.py:331
  41.7 3.3 %collective-permute-start.14 = (f32[1,128]{1,0:T(1,128)S(1)}, f32[1,128]{1,0:T(1,128)S(1)}, u32[]{:S(2)}, u32[]{:S(2)}) collective-permute-start(f32[1,128]{1,0:T(1,128)S(1)} %add.10), channel_id=1, source_target_pairs={{0,4},{2,6},{4,0},{6,2},{1,5},{3,7},{5,1},{7,3},{8,12},{10,14},{12... | collective-permute-start | bytes 1544 | tf_op jit(solution)/shard_map/ppermute | solution.py:331
  45.0 0.7 %finish.1 = bf16[128,256]{1,0:T(8,128)(2,1)} custom-call(f32[128,256]{1,0:T(8,128)S(1)} %get-tuple-element.22.refs_0_, bf16[128,256]{1,0:T(8,128)(2,1)S(1)} %collective-permute-done.6.refs_1_, bf16[128,256]{1,0:T(8,128)(2,1)S(1)} %collective-permute-done.7.refs_2_, bf16[128,256]{1,0:T(8,128)(2,1)S(1)} %collective-permute-done.8.refs_3_), custom_call_target="tpu_custom_call" | custom-call | tf_op jit(solution)/shard_map/finish/pallas_call | solution.py:303
  45.7 0.9 %collective-permute-done.14 = f32[1,128]{1,0:T(1,128)S(1)} collective-permute-done((f32[1,128]{1,0:T(1,128)S(1)}, f32[1,128]{1,0:T(1,128)S(1)}, u32[]{:S(2)}, u32[]{:S(2)}) %collective-permute-start.14) | collective-permute-done | bytes 544 | tf_op jit(solution)/shard_map/ppermute | solution.py:331
  46.6 0.5 %add.11 = f32[1,128]{1,0:T(1,128)} add(f32[1,128]{1,0:T(1,128)S(1)} %add.10, f32[1,128]{1,0:T(1,128)S(1)} %collective-permute-done.14) | non-fusion elementwise | flops 128 | bytes 1536 | tf_op jit(solution)/shard_map/add | solution.py:363
  (28 shorter events, 0.1 us)
Async XLA Ops:
  0.6 5.8 %copy-start.8 = (f32[1,32]{1,0:T(1,128)S(1)}, f32[1,32]{1,0:T(1,128)}, u32[]{:S(2)}) copy-start(f32[1,32]{1,0:T(1,128)} %coef.1) | copy-start | bytes 388
  0.6 5.8 %copy-start.9 = (s32[1,8]{1,0:T(1,128)S(1)}, s32[1,8]{1,0:T(1,128)}, u32[]{:S(2)}) copy-start(s32[1,8]{1,0:T(1,128)} %mask.1) | copy-start | bytes 100
  0.7 5.8 %copy-start.6 = (s32[1,8,128]{2,1,0:T(8,128)S(1)}, s32[1,8,128]{2,1,0:T(8,128)}, u32[]{:S(2)}) copy-start(s32[1,8,128]{2,1,0:T(8,128)} %src.1) | copy-start | bytes 12292
  0.7 5.8 %copy-start.7 = (s32[1,8,128]{2,1,0:T(8,128)S(1)}, s32[1,8,128]{2,1,0:T(8,128)}, u32[]{:S(2)}) copy-start(s32[1,8,128]{2,1,0:T(8,128)} %dst.3) | copy-start | bytes 12292
  0.7 5.8 %copy-start.4 = (bf16[1024,512]{1,0:T(8,128)(2,1)S(1)}, bf16[1024,512]{1,0:T(8,128)(2,1)}, u32[]{:S(2)}) copy-start(bf16[1024,512]{1,0:T(8,128)(2,1)} %table.1) | copy-start | bytes 3145732
  0.7 5.8 %copy-start.5 = (bf16[1,8,128,128]{3,2,1,0:T(8,128)(2,1)S(1)}, bf16[1,8,128,128]{3,2,1,0:T(8,128)(2,1)}, u32[]{:S(2)}) copy-start(bf16[1,8,128,128]{3,2,1,0:T(8,128)(2,1)} %weights.1) | copy-start | bytes 786436
  0.7 5.8 %copy-start.3 = (bf16[32,512,256]{2,1,0:T(8,128)(2,1)S(1)}, bf16[32,512,256]{2,1,0:T(8,128)(2,1)}, u32[]{:S(2)}) copy-start(bf16[32,512,256]{2,1,0:T(8,128)(2,1)} %basis.3) | copy-start | bytes 25165828
  0.7 9.8 %collective-permute-start = (bf16[128,256]{1,0:T(8,128)(2,1)}, bf16[128,256]{1,0:T(8,128)(2,1)S(1)}, u32[]{:S(2)}, u32[]{:S(2)}) collective-permute-start(bf16[128,256]{1,0:T(8,128)(2,1)} %refs_0_.1), channel_id=1, source_target_pairs={{0,2},{2,0},{4,6},{6,4},{1,3},{3,1},{5,7},{7,5},{8,10},{10,8},{12,... | collective-permute-start | bytes 196616 | tf_op jit(solution)/shard_map/ppermute | solution.py:331
  3.8 7.5 %collective-permute-start.1 = (bf16[128,256]{1,0:T(8,128)(2,1)}, bf16[128,256]{1,0:T(8,128)(2,1)S(1)}, u32[]{:S(2)}, u32[]{:S(2)}) collective-permute-start(bf16[128,256]{1,0:T(8,128)(2,1)} %refs_0_.1), channel_id=1, source_target_pairs={{0,4},{2,6},{4,0},{6,2},{1,5},{3,7},{5,1},{7,3},{8,12},{10,14},{12... | collective-permute-start | bytes 196616 | tf_op jit(solution)/shard_map/ppermute | solution.py:331
  6.4 6.3 %collective-permute-start.2 = (bf16[128,256]{1,0:T(8,128)(2,1)}, bf16[128,256]{1,0:T(8,128)(2,1)S(1)}, u32[]{:S(2)}, u32[]{:S(2)}) collective-permute-start(bf16[128,256]{1,0:T(8,128)(2,1)} %refs_0_.1), channel_id=1, source_target_pairs={{0,6},{2,4},{4,2},{6,0},{1,7},{3,5},{5,3},{7,1},{8,14},{10,12},{12... | collective-permute-start | bytes 196616 | tf_op jit(solution)/shard_map/ppermute | solution.py:331
  6.5 6.2 %copy-start = (bf16[128,256]{1,0:T(8,128)(2,1)S(1)}, bf16[128,256]{1,0:T(8,128)(2,1)}, u32[]{:S(2)}) copy-start(bf16[128,256]{1,0:T(8,128)(2,1)} %refs_0_.1) | copy-start | bytes 196612
  6.5 6.2 %copy-start.1 = (f32[4,256]{1,0:T(4,128)S(1)}, f32[4,256]{1,0:T(4,128)}, u32[]{:S(2)}) copy-start(f32[4,256]{1,0:T(4,128)} %bias.1) | copy-start | bytes 12292
  6.5 6.2 %copy-start.2 = (s32[4]{0:T(128)S(1)}, s32[4]{0:T(128)}, u32[]{:S(2)}) copy-start(s32[4]{0:T(128)} %type_rows.1) | copy-start | bytes 52
  13.3 6.5 %collective-permute-start.10 = (bf16[512,256]{1,0:T(8,128)(2,1)S(1)}, bf16[512,256]{1,0:T(8,128)(2,1)S(1)}, u32[]{:S(2)}, u32[]{:S(2)}) collective-permute-start(bf16[512,256]{1,0:T(8,128)(2,1)S(1)} %get-tuple-element.26.rest_0_), channel_id=1, source_target_pairs={{0,16},{8,24},{16,0},{24,8},{1,17},{9,25},{17,1},{25,9},{2,18},{10... | collective-permute-start | bytes 786440 | tf_op jit(solution)/shard_map/ppermute | solution.py:331
  14.9 15.9 %collective-permute-start.9 = (bf16[512,256]{1,0:T(8,128)(2,1)S(1)}, bf16[512,256]{1,0:T(8,128)(2,1)S(1)}, u32[]{:S(2)}, u32[]{:S(2)}) collective-permute-start(bf16[512,256]{1,0:T(8,128)(2,1)S(1)} %get-tuple-element.26.rest_0_), channel_id=1, source_target_pairs={{0,8},{8,0},{16,24},{24,16},{1,9},{9,1},{17,25},{25,17},{2,10},{10... | collective-permute-start | bytes 786440 | tf_op jit(solution)/shard_map/ppermute | solution.py:331
  14.9 8.9 %collective-permute-start.3 = (bf16[272,256]{1,0:T(8,128)(2,1)S(1)}, bf16[272,256]{1,0:T(8,128)(2,1)S(1)}, u32[]{:S(2)}, u32[]{:S(2)}) collective-permute-start(bf16[272,256]{1,0:T(8,128)(2,1)S(1)} %get-tuple-element.19), channel_id=1, source_target_pairs={{0,2},{2,0},{4,6},{6,4},{1,3},{3,1},{5,7},{7,5},{8,10},{10,8},{12,... | collective-permute-start | bytes 417800 | tf_op jit(solution)/shard_map/ppermute | solution.py:331
  14.9 13.5 %collective-permute-start.4 = (bf16[272,256]{1,0:T(8,128)(2,1)S(1)}, bf16[272,256]{1,0:T(8,128)(2,1)S(1)}, u32[]{:S(2)}, u32[]{:S(2)}) collective-permute-start(bf16[272,256]{1,0:T(8,128)(2,1)S(1)} %get-tuple-element.20), channel_id=1, source_target_pairs={{0,4},{2,6},{4,0},{6,2},{1,5},{3,7},{5,1},{7,3},{8,12},{10,14},{12... | collective-permute-start | bytes 417800 | tf_op jit(solution)/shard_map/ppermute | solution.py:331
  17.2 11.1 %collective-permute-start.5 = (bf16[272,256]{1,0:T(8,128)(2,1)S(1)}, bf16[272,256]{1,0:T(8,128)(2,1)S(1)}, u32[]{:S(2)}, u32[]{:S(2)}) collective-permute-start(bf16[272,256]{1,0:T(8,128)(2,1)S(1)} %get-tuple-element.21), channel_id=1, source_target_pairs={{0,6},{2,4},{4,2},{6,0},{1,7},{3,5},{5,3},{7,1},{8,14},{10,12},{12... | collective-permute-start | bytes 417800 | tf_op jit(solution)/shard_map/ppermute | solution.py:331
  19.8 12.2 %collective-permute-start.11 = (bf16[512,256]{1,0:T(8,128)(2,1)S(1)}, bf16[512,256]{1,0:T(8,128)(2,1)S(1)}, u32[]{:S(2)}, u32[]{:S(2)}) collective-permute-start(bf16[512,256]{1,0:T(8,128)(2,1)S(1)} %collective-permute-done.10.rest_2_), channel_id=1, source_target_pairs={{0,8},{8,0},{16,24},{24,16},{1,9},{9,1},{17,25},{25,17},{2,10},{10... | collective-permute-start | bytes 786440 | tf_op jit(solution)/shard_map/ppermute | solution.py:331
  28.8 16.2 %collective-permute-start.6 = (bf16[128,256]{1,0:T(8,128)(2,1)S(1)}, bf16[128,256]{1,0:T(8,128)(2,1)S(1)}, u32[]{:S(2)}, u32[]{:S(2)}) collective-permute-start(bf16[128,256]{1,0:T(8,128)(2,1)S(1)} %get-tuple-element.23), channel_id=1, source_target_pairs={{0,8},{8,0},{16,24},{24,16},{1,9},{9,1},{17,25},{25,17},{2,10},{10... | collective-permute-start | bytes 196616 | tf_op jit(solution)/shard_map/ppermute | solution.py:331
  28.9 16.1 %collective-permute-start.7 = (bf16[128,256]{1,0:T(8,128)(2,1)S(1)}, bf16[128,256]{1,0:T(8,128)(2,1)S(1)}, u32[]{:S(2)}, u32[]{:S(2)}) collective-permute-start(bf16[128,256]{1,0:T(8,128)(2,1)S(1)} %get-tuple-element.24), channel_id=1, source_target_pairs={{0,16},{8,24},{16,0},{24,8},{1,17},{9,25},{17,1},{25,9},{2,18},{10... | collective-permute-start | bytes 196616 | tf_op jit(solution)/shard_map/ppermute | solution.py:331
  29.5 15.6 %collective-permute-start.8 = (bf16[128,256]{1,0:T(8,128)(2,1)S(1)}, bf16[128,256]{1,0:T(8,128)(2,1)S(1)}, u32[]{:S(2)}, u32[]{:S(2)}) collective-permute-start(bf16[128,256]{1,0:T(8,128)(2,1)S(1)} %get-tuple-element.25), channel_id=1, source_target_pairs={{0,24},{8,16},{16,8},{24,0},{1,25},{9,17},{17,9},{25,1},{2,26},{10... | collective-permute-start | bytes 196616 | tf_op jit(solution)/shard_map/ppermute | solution.py:331
  33.5 3.6 %collective-permute-start.12 = (f32[1,128]{1,0:T(1,128)S(1)}, f32[1,128]{1,0:T(1,128)S(1)}, u32[]{:S(2)}, u32[]{:S(2)}) collective-permute-start(f32[1,128]{1,0:T(1,128)S(1)} %grad.1), channel_id=1, source_target_pairs={{0,1},{1,0},{2,3},{3,2},{4,5},{5,4},{6,7},{7,6},{8,9},{9,8},{10,11... | collective-permute-start | bytes 1544 | tf_op jit(solution)/shard_map/ppermute | solution.py:331
  37.1 4.6 %collective-permute-start.13 = (f32[1,128]{1,0:T(1,128)S(1)}, f32[1,128]{1,0:T(1,128)S(1)}, u32[]{:S(2)}, u32[]{:S(2)}) collective-permute-start(f32[1,128]{1,0:T(1,128)S(1)} %add.9), channel_id=1, source_target_pairs={{0,2},{2,0},{4,6},{6,4},{1,3},{3,1},{5,7},{7,5},{8,10},{10,8},{12,... | collective-permute-start | bytes 1544 | tf_op jit(solution)/shard_map/ppermute | solution.py:331
  41.7 4.8 %collective-permute-start.14 = (f32[1,128]{1,0:T(1,128)S(1)}, f32[1,128]{1,0:T(1,128)S(1)}, u32[]{:S(2)}, u32[]{:S(2)}) collective-permute-start(f32[1,128]{1,0:T(1,128)S(1)} %add.10), channel_id=1, source_target_pairs={{0,4},{2,6},{4,0},{6,2},{1,5},{3,7},{5,1},{7,3},{8,12},{10,14},{12... | collective-permute-start | bytes 1544 | tf_op jit(solution)/shard_map/ppermute | solution.py:331
